TPU v7x, 32 devices: a whole 2x2x4 slice. The times are simulated.
32 devices in a mesh: seq: 8 (over z, y), ch: 4 (over x, core).
Axes of the slice: x: 2, y: 2, z: 4, core: 2. Of those that a mesh axis runs over, the one named last changes fastest.
Arguments:
- signal: float32 [1, 65536, 1024], P(None, 'seq', 'ch'), may hold values from -6 to 6
- spectrum: float32 [2, 256, 256, 1024], P(None, 'seq', None, 'ch'), may hold values from -6 to 6
- channel_mode: int32 [1024], P('ch'), may hold values 0 or 1
- skip_gain: float32 [1024], P('ch'), may hold values from -4 to 4
- out_weight: bfloat16 [1024, 1024], P('ch'), may hold values from -0.1875 to 0.1875
Outputs:
- projected: float32 [1, 65536, 1024], P(None, 'seq', 'ch')
Inputs may be any that keep to these rules, and one draw needn't show every extreme that they name: `channel_mode`: 1 marks a channel whose 65536 positions are one sequence, 0 a channel whose positions form a 256 x 256 image.
All inputs are finite; a program needn't handle non-finite values. No bound on the sum of `channel_mode` on one device may be relied on, other than what follows from the above.
Results may differ from a plain program's by a relative error of at most 0.017.
Values may be sent and summed in bfloat16 or wider, within the bound.
No kernel may reach another device: no remote copies, remote signals or barrier semaphores. Data moves between devices by JAX's collectives and lax.ppermute only.
A program may use at most 192 MiB of HBM per device.

v0:
```python
import math
import jax
import jax.numpy as jnp
from jax import lax
from jax.sharding import PartitionSpec as P

ROWS = 256
COLUMNS = 256
LENGTH = 65536


def contract(pattern, operand, matrix):
    return jnp.einsum(
        pattern,
        operand,
        matrix,
        precision=lax.Precision.HIGHEST,
        preferred_element_type=jnp.float32,
    )


def phase_table(row_index, col_index, period):
    product = row_index[:, None] * col_index[None, :] % period
    angles = product.astype(jnp.float32) * (2.0 * math.pi / period)
    return (jnp.cos(angles), jnp.sin(angles))


def square_table(length):
    counter = jnp.arange(length, dtype=jnp.int32)
    return phase_table(counter, counter, length)


def transform_real(pattern, operand, cosine_table, sine_table):
    return (contract(pattern, operand, cosine_table), -contract(pattern, operand, sine_table))


def transform_complex(pattern, real_part, imag_part, cosine_table, sine_table, orient):
    real_out = contract(pattern, real_part, cosine_table) - orient * contract(
        pattern, imag_part, sine_table
    )
    imag_out = orient * contract(pattern, real_part, sine_table) + contract(
        pattern, imag_part, cosine_table
    )
    return (real_out, imag_out)


def inverse_real(pattern, real_part, imag_part, cosine_table, sine_table, factor):
    return (
        contract(pattern, real_part, cosine_table) - contract(pattern, imag_part, sine_table)
    ) * factor


def rotate(real_part, imag_part, cosine_table, sine_table, orient):
    real_out = real_part * cosine_table - orient * imag_part * sine_table
    imag_out = orient * real_part * sine_table + imag_part * cosine_table
    return (real_out, imag_out)


def filter_product(real_part, imag_part, filter_real, filter_imag):
    return (
        real_part * filter_real - imag_part * filter_imag,
        real_part * filter_imag + imag_part * filter_real,
    )


def channel_plan(signal, spectrum, channel_mode):
    groups = lax.axis_size("seq")
    position = lax.axis_index("seq")
    batches, local_len, owned = signal.shape
    rows_local = ROWS // groups
    shared = owned // groups
    tiled = signal.reshape(batches, rows_local, COLUMNS, owned)
    gathered, filters = (
        lax.all_to_all(
            tiled.astype(jnp.bfloat16), "seq", split_axis=3, concat_axis=1, tiled=True
        ).astype(tiled.dtype),
        lax.all_to_all(
            spectrum.astype(jnp.bfloat16), "seq", split_axis=3, concat_axis=1, tiled=True
        ).astype(spectrum.dtype),
    )
    own_modes = lax.dynamic_slice_in_dim(channel_mode, position * shared, shared)
    selector = (own_modes == 1)[None, :, None, None]
    images = jnp.transpose(gathered, (0, 3, 1, 2))
    filters_first = jnp.transpose(filters, (0, 3, 1, 2))
    row_cos, row_sin = square_table(ROWS)
    col_cos, col_sin = square_table(COLUMNS)
    twist_cos, twist_sin = phase_table(
        jnp.arange(ROWS, dtype=jnp.int32), jnp.arange(COLUMNS, dtype=jnp.int32), LENGTH
    )
    chosen_cos = jnp.where(selector, twist_cos[None, None], 1.0)
    chosen_sin = jnp.where(selector, twist_sin[None, None], 0.0)
    real_part, imag_part = transform_real("xmab,ad->xmdb", images, row_cos, row_sin)
    real_part, imag_part = rotate(real_part, imag_part, chosen_cos, chosen_sin, -1.0)
    real_part, imag_part = transform_complex(
        "xmdb,bc->xmdc", real_part, imag_part, col_cos, col_sin, -1.0
    )
    real_part, imag_part = filter_product(
        real_part, imag_part, filters_first[0][None], filters_first[1][None]
    )
    real_part, imag_part = transform_complex(
        "xmdc,cb->xmdb", real_part, imag_part, col_cos, col_sin, 1.0
    )
    real_part, imag_part = rotate(real_part, imag_part, chosen_cos, chosen_sin, 1.0)
    convolved = inverse_real("xmdb,da->xmab", real_part, imag_part, row_cos, row_sin, 1.0 / LENGTH)
    convolved = jnp.transpose(convolved, (0, 2, 3, 1))
    restored = lax.all_to_all(
        convolved.astype(jnp.bfloat16), "seq", split_axis=1, concat_axis=3, tiled=True
    ).astype(convolved.dtype)
    return restored.reshape(batches, local_len, owned)


def per_device(signal, spectrum, channel_mode, skip_gain, out_weight):
    convolved = channel_plan(signal, spectrum, channel_mode)
    hidden = (convolved + skip_gain[None, None, :] * signal).astype(jnp.bfloat16)
    partials = jnp.einsum("xtc,cj->xtj", hidden, out_weight, preferred_element_type=jnp.float32)
    return lax.psum_scatter(
        partials.astype(jnp.bfloat16), "ch", scatter_dimension=2, tiled=True
    ).astype(jnp.float32)


def solution(mesh):
    placed = (P(None, "seq", "ch"), P(None, "seq", None, "ch"), P("ch"), P("ch"), P("ch", None))
    return jax.shard_map(
        per_device, mesh=mesh, in_specs=placed, out_specs=P(None, "seq", "ch"), check_vma=False
    )
```

profile of v0, /device:TPU:0, one launch (start us, length us, event | category | flops | bytes accessed | tf_op | source)
XLA Modules:
  0.0 736.7 jit_solution(1022630028297481340)
XLA Ops:
  6.5 0.0 copy-start
  6.5 5.9 convert_element_type.113
  12.4 7.9 %copy.55 = bf16[1,32,256,256]{2,1,0,3:T(8,128)(2,1)} copy(bf16[1,32,256,256]{3,2,1,0:T(8,128)(2,1)} %bitcast.140) | data formatting | bytes 8388608 | tf_op jit(solution)/shard_map/convert_element_type | solution.py:75
  20.3 7.3 all-to-all-start
  27.6 16.8 %copy.62 = bf16[2,32,256,256]{2,1,0,3:T(8,128)(2,1)} copy(f32[2,32,256,256]{3,2,1,0:T(8,128)} %param.6) | data formatting | bytes 25165824 | tf_op args[1]
  44.5 76.5 %all-to-all-done = bf16[1,32,256,256]{2,1,0,3:T(8,128)(2,1)} async-done(((bf16[1,32,256,256]{2,1,0,3:T(8,128)(2,1)}), bf16[1,32,256,256]{2,1,0,3:T(8,128)(2,1)}, u32[]{:S(2)}, u32[]{:S(2)}) %all-to-all-start) | async-done | bytes 4194336 | tf_op jit(solution)/shard_map/all_to_all | solution.py:74
  120.9 5.0 all-to-all-start.1
  125.9 1.0 fusion.67
  126.9 0.1 copy.59
  127.0 1.0 fusion.68
  128.0 0.1 copy.58
  128.1 0.0 copy-done.5
  128.1 0.1 dynamic-slice_compare_fusion
  128.2 4.6 copy.56
  132.8 2.4 copy.57
  135.2 4.8 fusion.58
  140.0 0.0 copy-start.1
  140.0 5.0 fusion.50
  145.0 0.0 copy-start.2
  145.0 11.7 %fusion.55 = f32[32,256,256]{2,1,0:T(8,128)} fusion(f32[256,32,256]{2,0,1:T(8,128)S(1)} %fusion.58, f32[256,32,256]{2,0,1:T(8,128)S(1)} %fusion.50, f32[256,256]{1,0:T(8,128)S(1)} %copy.59, f32[256,256]{1,0:T(8,128)S(1)} %copy.58, pred[32]{0:T(512)(128)(4,1)S(1)} %dynamic-slice_compare_fusion), kind=kOutput, calls=%fused_computation.76 | convolution fusion | flops 6458048512 | bytes 25690144 | tf_op jit(solution)/shard_map/xmdb,bc->xmdc/dot_general | solution.py:13
  156.7 12.0 %fusion.46 = f32[32,256,256]{2,1,0:T(8,128)} fusion(f32[256,32,256]{2,0,1:T(8,128)S(1)} %fusion.58, f32[256,32,256]{2,0,1:T(8,128)S(1)} %fusion.50, f32[256,256]{1,0:T(8,128)S(1)} %copy.59, f32[256,256]{1,0:T(8,128)S(1)} %copy.58, pred[32]{0:T(512)(128)(4,1)S(1)} %dynamic-slice_compare_fusion), kind=kOutput, calls=%fused_computation.67 | convolution fusion | flops 6458048512 | bytes 25690144 | tf_op jit(solution)/shard_map/xmdb,bc->xmdc/dot_general | solution.py:13
  168.6 0.0 copy-done.1
  168.6 0.0 copy-done.2
  168.6 14.4 %multiply_subtract_fusion = f32[32,256,256]{2,1,0:T(8,128)} fusion(f32[32,256,256]{2,1,0:T(8,128)} %fusion.55, f32[256,32,256]{2,0,1:T(8,128)S(1)} %fusion.58, f32[256,32,256]{2,0,1:T(8,128)S(1)} %fusion.50, f32[256,256]{1,0:T(8,128)S(1)} %copy.59, f32[256,256]{1,0:T(8,128)S(1)} %copy.58, pred[32]{0:T(512)(128)(4,1)S(1)} %dynamic-slice_compare_fusion), kind=kOutput, calls=%fused_computation.38 | convolution fusion | flops 6462242816 | bytes 34078752 | tf_op jit(solution)/shard_map/xmdb,bc->xmdc/dot_general | solution.py:13
  183.0 125.1 %all-to-all-done.1 = bf16[2,32,256,256]{2,1,0,3:T(8,128)(2,1)} async-done(((bf16[2,32,256,256]{2,1,0,3:T(8,128)(2,1)}), bf16[2,32,256,256]{2,1,0,3:T(8,128)(2,1)}, u32[]{:S(2)}, u32[]{:S(2)}) %all-to-all-start.1) | async-done | bytes 8388640 | tf_op jit(solution)/shard_map/all_to_all | solution.py:77
  308.1 11.4 %copy.63 = bf16[2,32,256,256]{2,3,1,0:T(8,128)(2,1)} copy(bf16[2,32,256,256]{2,1,0,3:T(8,128)(2,1)} %all-to-all-done.1) | data formatting | bytes 16777216 | tf_op jit(solution)/shard_map/all_to_all | solution.py:77
  319.5 11.4 %convert_bitcast_fusion = f32[2,8,32,256,32]{3,4,1,2,0:T(8,128)} fusion(bf16[2,32,256,8,32]{2,4,3,1,0:T(8,128)(2,1)} %bitcast.138), kind=kLoop, calls=%fused_computation | loop fusion | flops 4194304 | bytes 25165824 | tf_op jit(solution)/shard_map/transpose | solution.py:84
  330.9 17.8 %copy.64 = f32[2,8,32,256,32]{3,2,1,4,0:T(8,128)} copy(f32[2,8,32,256,32]{3,4,1,2,0:T(8,128)} %convert_bitcast_fusion) | data formatting | bytes 33554432 | tf_op jit(solution)/shard_map/transpose | solution.py:84
  348.7 27.1 %fusion.19 = (f32[1,32,256,256]{3,2,1,0:T(8,128)}, f32[1,32,256,256]{3,2,1,0:T(8,128)}) fusion(f32[32,256,256]{2,1,0:T(8,128)} %multiply_subtract_fusion, f32[2,32,256,256]{3,2,1,0:T(8,128)} %bitcast.137, f32[256,32,256]{2,0,1:T(8,128)} %copy-done.1, f32[256,32,256]{2,0,1:T(8,128)} %copy-done.2, f32[256,256]{1,0:T(8,128)S(1)} %copy.59, ...), kind=kOutput, calls=%fused_computation.29 | convolution fusion | flops 6474825728 | bytes 67633184 | tf_op jit(solution)/shard_map/xmdb,bc->xmdc/dot_general | solution.py:13
  375.8 13.2 %fusion.14 = f32[32,256,256]{2,1,0:T(8,128)} fusion(f32[1,32,256,256]{3,2,1,0:T(8,128)} %get-tuple-element.6), kind=kOutput, calls=%fused_computation.22 | convolution fusion | flops 6443368448 | bytes 16777216 | tf_op jit(solution)/shard_map/xmdc,cb->xmdb/dot_general | solution.py:13
  389.0 0.0 copy-done.3
  389.0 11.2 %fusion.16 = f32[32,256,256]{2,1,0:T(8,128)} fusion(f32[1,32,256,256]{3,2,1,0:T(8,128)S(1)} %copy-done.3), kind=kOutput, calls=%fused_computation.24 | convolution fusion | flops 6443368448 | bytes 16777216 | tf_op jit(solution)/shard_map/xmdc,cb->xmdb/dot_general | solution.py:13
  400.1 10.8 %fusion.10 = f32[32,256,256]{2,1,0:T(8,128)} fusion(f32[1,32,256,256]{3,2,1,0:T(8,128)S(1)} %bitcast.134), kind=kOutput, calls=%fused_computation.18 | convolution fusion | flops 6443368448 | bytes 16777216 | tf_op jit(solution)/shard_map/xmdc,cb->xmdb/dot_general | solution.py:13
  411.0 11.0 %fusion.12 = f32[32,256,256]{2,1,0:T(8,128)} fusion(f32[1,32,256,256]{3,2,1,0:T(8,128)S(1)} %bitcast.134), kind=kOutput, calls=%fused_computation.20 | convolution fusion | flops 6443368448 | bytes 16777216 | tf_op jit(solution)/shard_map/xmdc,cb->xmdb/dot_general | solution.py:13
  422.0 19.1 %fusion.5 = f32[256,32,256]{2,0,1:T(8,128)} fusion(f32[256,256]{1,0:T(8,128)S(1)} %copy.59, f32[256,256]{1,0:T(8,128)S(1)} %copy.58, pred[32]{0:T(512)(128)(4,1)S(1)} %dynamic-slice_compare_fusion, f32[32,256,256]{2,1,0:T(8,128)} %fusion.14, f32[32,256,256]{2,1,0:T(8,128)} %fusion.10, f32[32,256,256]{2,1,0:T(8,128)} %fusion.16, f32[32,256,256]{2,1,0:T(8,128)} %fusion.12), kind=kOutput, calls=%fused_computation.15 | convolution fusion | flops 6458048512 | bytes 42467360 | tf_op jit(solution)/shard_map/xmdb,da->xmab/dot_general | solution.py:13
  441.1 20.9 %fusion.20 = bf16[1,256,256,32]{2,1,3,0:T(8,128)(2,1)} fusion(f32[256,32,256]{2,0,1:T(8,128)} %fusion.5, f32[256,256]{1,0:T(8,128)S(1)} %copy.59, f32[256,256]{1,0:T(8,128)S(1)} %copy.58, pred[32]{0:T(512)(128)(4,1)S(1)} %dynamic-slice_compare_fusion, f32[32,256,256]{2,1,0:T(8,128)} %fusion.14, f32[32,256,256]{2,1,0:T(8,128)} %fusion.10, ...), kind=kOutput, calls=%fused_computation.39 | convolution fusion | flops 6464339968 | bytes 46661664 | tf_op jit(solution)/shard_map/xmdb,da->xmab/dot_general | solution.py:13
  461.9 6.6 copy.73
  468.5 4.5 all-to-all-start.2
  473.1 0.0 reduce-scatter.2.cloned.1.call-start
  473.1 9.2 %copy.75 = f32[1,8192,256]{1,2,0:T(8,128)} copy(f32[1,8192,256]{2,1,0:T(8,128)} %param.5) | data formatting | bytes 16777216 | tf_op args[0]
  482.3 83.3 %all-to-all-done.2 = bf16[1,256,256,32]{2,3,0,1:T(8,128)(2,1)} async-done(((bf16[1,256,256,32]{2,3,0,1:T(8,128)(2,1)}), bf16[1,256,256,32]{2,3,0,1:T(8,128)(2,1)}, u32[]{:S(2)}, u32[]{:S(2)}) %all-to-all-start.2) | async-done | bytes 4194336 | tf_op jit(solution)/shard_map/all_to_all | solution.py:106
  565.6 8.0 %copy.93 = f32[1,8,32,256,32]{3,2,4,1,0:T(8,128)} copy(bf16[1,8,32,256,32]{3,4,2,1,0:T(8,128)(2,1)} %bitcast.44) | data formatting | bytes 12582912 | tf_op jit(solution)/shard_map/convert_element_type | solution.py:108
  573.6 9.4 %reshape.154 = f32[1,8192,256]{1,2,0:T(8,128)} reshape(f32[1,32,256,8,32]{2,1,4,3,0:T(8,128)} %bitcast.139) | data formatting | bytes 16777216 | tf_op jit(solution)/shard_map/convert_element_type | solution.py:108
  583.0 0.0 copy-done
  583.0 16.1 %convert_bitcast_fusion.1 = bf16[1,8192,1024]{2,1,0:T(8,128)(2,1)} fusion(bf16[256,1024]{1,0:T(8,128)(2,1)S(1)} %copy-done, f32[1,8192,256]{1,2,0:T(8,128)} %reshape.154, f32[1,8192,256]{1,2,0:T(8,128)} %copy.75, f32[256]{0:T(256)S(1)} %copy-done.4), kind=kOutput, calls=%fused_computation.1 | convolution fusion | flops 4309647360 | bytes 34079744 | tf_op jit(solution)/shard_map/xtc,cj->xtj/dot_general | solution.py:115
  599.1 0.0 reduce-scatter.2.cloned.1.call-update
  599.2 124.0 %reduce-scatter.2.cloned.1.call-done = bf16[1,8192,256]{2,1,0:T(8,128)(2,1)} async-done(((bf16[1,8192,1024]{2,1,0:T(8,128)(2,1)}), bf16[1,8192,256]{2,1,0:T(8,128)(2,1)}) %reduce-scatter.2.cloned.1.call-update) | async-done | bytes 4194320 | tf_op jit(solution)/shard_map/reduce_scatter | solution.py:116
  723.2 6.2 convert_element_type.130
  (9 shorter events, 0.0 us)
Async XLA Ops:
  6.5 576.5 %copy-start = (bf16[256,1024]{1,0:T(8,128)(2,1)S(1)}, bf16[256,1024]{1,0:T(8,128)(2,1)}, u32[]{:S(2)}) copy-start(bf16[256,1024]{1,0:T(8,128)(2,1)} %param.9) | copy-start | bytes 1572868
  20.3 100.6 %all-to-all-start = ((bf16[1,32,256,256]{2,1,0,3:T(8,128)(2,1)}), bf16[1,32,256,256]{2,1,0,3:T(8,128)(2,1)}, u32[]{:S(2)}, u32[]{:S(2)}) async-start(bf16[1,32,256,256]{2,1,0,3:T(8,128)(2,1)} %copy.55), calls=%async_computation | async-start | bytes 8388608 | tf_op jit(solution)/shard_map/all_to_all | solution.py:74
  44.5 83.6 %copy-start.5 = (s32[256]{0:T(256)S(1)}, s32[256]{0:T(256)}, u32[]{:S(2)}) copy-start(s32[256]{0:T(256)} %param.7) | copy-start | bytes 3076
  120.9 187.2 %all-to-all-start.1 = ((bf16[2,32,256,256]{2,1,0,3:T(8,128)(2,1)}), bf16[2,32,256,256]{2,1,0,3:T(8,128)(2,1)}, u32[]{:S(2)}, u32[]{:S(2)}) async-start(bf16[2,32,256,256]{2,1,0,3:T(8,128)(2,1)} %copy.62), calls=%async_computation.1 | async-start | bytes 16777216 | tf_op jit(solution)/shard_map/all_to_all | solution.py:77
  140.0 28.7 %copy-start.1 = (f32[256,32,256]{2,0,1:T(8,128)}, f32[256,32,256]{2,0,1:T(8,128)S(1)}, u32[]{:S(2)}) copy-start(f32[256,32,256]{2,0,1:T(8,128)S(1)} %fusion.58) | copy-start | bytes 25165828
  145.0 23.6 %copy-start.2 = (f32[256,32,256]{2,0,1:T(8,128)}, f32[256,32,256]{2,0,1:T(8,128)S(1)}, u32[]{:S(2)}) copy-start(f32[256,32,256]{2,0,1:T(8,128)S(1)} %fusion.50) | copy-start | bytes 25165828
  375.8 13.2 %copy-start.3 = (f32[1,32,256,256]{3,2,1,0:T(8,128)S(1)}, f32[1,32,256,256]{3,2,1,0:T(8,128)}, u32[]{:S(2)}) copy-start(f32[1,32,256,256]{3,2,1,0:T(8,128)} %get-tuple-element.6) | copy-start | bytes 25165828
  375.8 24.4 %slice-start = ((s8[8388608]{0:T(1024)(128)(4,1)}), s8[4194304]{0:T(1024)(128)(4,1)S(1)}, s32[]{:S(2)}) async-start(s8[8388608]{0:T(1024)(128)(4,1)} %bitcast.133), calls=%async_computation.5 | async-start | bytes 8388608
  389.0 11.2 %slice-start.1 = ((s8[8388608]{0:T(1024)(128)(4,1)}), s8[4194304]{0:T(1024)(128)(4,1)S(1)}, s32[]{:S(2)}) async-start(s8[8388608]{0:T(1024)(128)(4,1)} %bitcast.133), calls=%async_computation.6 | async-start | bytes 8388608
  468.5 97.0 %all-to-all-start.2 = ((bf16[1,256,256,32]{2,3,0,1:T(8,128)(2,1)}), bf16[1,256,256,32]{2,3,0,1:T(8,128)(2,1)}, u32[]{:S(2)}, u32[]{:S(2)}) async-start(bf16[1,256,256,32]{2,3,0,1:T(8,128)(2,1)} %copy.73), calls=%async_computation.2 | async-start | bytes 8388608 | tf_op jit(solution)/shard_map/all_to_all | solution.py:106
  473.1 250.1 %reduce-scatter.2.cloned.1.call-start = ((), (), s32[]{:S(2)}) async-start(), calls=%async_computation.4 | async-start | bytes 20971520 | tf_op jit(solution)/shard_map/reduce_scatter | solution.py:116
  573.6 9.4 %copy-start.4 = (f32[256]{0:T(256)S(1)}, f32[256]{0:T(256)}, u32[]{:S(2)}) copy-start(f32[256]{0:T(256)} %param.8) | copy-start | bytes 3076
Sparse Core Ops, SparseCore 0:
  599.3 123.8 reduce-scatter.1
where the time goes:
time: 748 us; the launch traced here: 737 us
  waiting for transfers between devices  409 us (55%)
  matrix products  177 us (24%)
  local copies, waits for them, and re-layouts  94.4 us (13%)
  other arithmetic  25.5 us (3%)
  starting transfers between devices  16.9 us (2%)
  between operations  14 us (2%)
    dot_general x12, matrix products, contract(): jnp.einsum(pattern, operand, matrix, precision=lax.Precision.HIGHEST, pre...  161 us
    all_to_all x1, waiting for transfers between devices, channel_plan(): lax.all_to_all(spectrum.astype(jnp.bfloat16), 'seq', split_axis=3, concat...  125 us
    reduce_scatter x1, waiting for transfers between devices, per_device(): lax.psum_scatter(partials.astype(jnp.bfloat16), 'ch', scatter_dimension=2...  124 us
    all_to_all x1, waiting for transfers between devices, channel_plan(): lax.all_to_all(convolved.astype(jnp.bfloat16), 'seq', split_axis=1, conca...  83.3 us
    all_to_all x1, waiting for transfers between devices, channel_plan(): lax.all_to_all(tiled.astype(jnp.bfloat16), 'seq', split_axis=3, concat_ax...  76.5 us
    unnamed x18, local copies, waits for them, and re-layouts  26 us
    transpose x1, local copies, waits for them, and re-layouts, channel_plan(): filters_first = jnp.transpose(filters, (0, 3, 1, 2))  17.8 us
    convert_element_type x2, local copies, waits for them, and re-layouts, channel_plan(): restored = lax.all_to_all(convolved.astype(jnp.bfloat16), 'seq', split_ax...  17.4 us
  transfers between devices with their start and end apart: 4, of which 4 were waited for; matrix products, arithmetic and copies ran while one was open for 11% of the time, Pallas kernels for 0%

commit v1 on v0

--- a/solution.py
+++ b/solution.py
@@ -7,6 +7,15 @@
 ROWS = 256
 COLUMNS = 256
 LENGTH = 65536
+
+
+def bring_types_by_axis(values, chip_axis):
+    return jnp.concatenate(
+        jax.lax.all_to_all(
+            jnp.stack(jnp.split(values, jax.lax.axis_size(chip_axis), axis=3)), chip_axis, 0, 0
+        ),
+        axis=1,
+    )
 
 
 def contract(pattern, operand, matrix):
@@ -71,9 +80,7 @@
     shared = owned // groups
     tiled = signal.reshape(batches, rows_local, COLUMNS, owned)
     gathered, filters = (
-        lax.all_to_all(
-            tiled.astype(jnp.bfloat16), "seq", split_axis=3, concat_axis=1, tiled=True
-        ).astype(tiled.dtype),
+        bring_types_by_axis(tiled.astype(jnp.bfloat16), "seq").astype(tiled.dtype),
         lax.all_to_all(
             spectrum.astype(jnp.bfloat16), "seq", split_axis=3, concat_axis=1, tiled=True
         ).astype(spectrum.dtype),

time: 748 us -> 775 us (1.036)
  local copies, waits for them, and re-layouts: 94.4 us -> 122 us
    unnamed x18 -> x33, local copies, waits for them, and re-layouts: 26 us -> 57.4 us
    convert_element_type x1 -> x0, local copies, waits for them, and re-layouts: 7.93 us -> none  [channel_plan(): tiled.astype(jnp.bfloat16)]
  transfers between devices with their start and end apart: 4 -> 4, of which waited for: 4 -> 4; matrix products, arithmetic and copies ran while one was open for 11% -> 10% of each run, Pallas kernels for 0% -> 0%
where the time goes in v1:
time: 775 us; the launch traced here: 767 us
  waiting for transfers between devices  413 us (53%)
  matrix products  177 us (23%)
  local copies, waits for them, and re-layouts  122 us (16%)
  other arithmetic  23.5 us (3%)
  starting transfers between devices  17 us (2%)
  between operations  13.8 us (2%)
    dot_general x12, matrix products, contract(): jnp.einsum(pattern, operand, matrix, precision=lax.Precision.HIGHEST, pre...  161 us
    all_to_all x1, waiting for transfers between devices, channel_plan(): lax.all_to_all(spectrum.astype(jnp.bfloat16), 'seq', split_axis=3, concat...  130 us
    reduce_scatter x1, waiting for transfers between devices, per_device(): lax.psum_scatter(partials.astype(jnp.bfloat16), 'ch', scatter_dimension=2...  124 us
    all_to_all x1, waiting for transfers between devices, channel_plan(): lax.all_to_all(convolved.astype(jnp.bfloat16), 'seq', split_axis=1, conca...  83.2 us
    all_to_all x1, waiting for transfers between devices, bring_types_by_axis(): jax.lax.all_to_all(jnp.stack(jnp.split(values, jax.lax.axis_size(chip_axi...  76.4 us
    unnamed x33, local copies, waits for them, and re-layouts  57.4 us
    transpose x1, local copies, waits for them, and re-layouts, channel_plan(): filters_first = jnp.transpose(filters, (0, 3, 1, 2))  17.8 us
    convert_element_type x2, local copies, waits for them, and re-layouts, channel_plan(): restored = lax.all_to_all(convolved.astype(jnp.bfloat16), 'seq', split_ax...  17.4 us
  transfers between devices with their start and end apart: 4, of which 4 were waited for; matrix products, arithmetic and copies ran while one was open for 10% of the time, Pallas kernels for 0%

profile of v1, /device:TPU:0, one launch (start us, length us, event | category | flops | bytes accessed | tf_op | source)
XLA Modules:
  0.0 767.3 jit_solution(16719556671051534170)
XLA Ops:
  6.5 3.8 convert_element_type.113
  10.4 7.2 fusion.139
  17.6 2.1 copy.89
  20.5 2.9 copy.90
  23.4 2.8 copy.91
  26.2 2.8 copy.92
  29.1 2.9 copy.93
  31.9 2.8 copy.94
  34.8 2.1 copy.95
  36.9 1.8 copy.96
  38.7 1.9 bitcast_dynamic-update-slice_fusion.6
  40.6 1.9 bitcast_dynamic-update-slice_fusion.5
  42.4 1.9 bitcast_dynamic-update-slice_fusion.4
  44.3 1.9 bitcast_dynamic-update-slice_fusion.3
  46.2 1.9 bitcast_dynamic-update-slice_fusion.2
  48.9 1.9 bitcast_dynamic-update-slice_fusion
  50.7 7.3 all-to-all-start
  58.1 16.9 %copy.58 = bf16[2,32,256,256]{2,1,0,3:T(8,128)(2,1)} copy(f32[2,32,256,256]{3,2,1,0:T(8,128)} %param.6) | data formatting | bytes 25165824 | tf_op args[1]
  74.9 76.4 %all-to-all-done = bf16[8,1,32,256,32]{3,2,4,1,0:T(8,128)(2,1)} async-done(((bf16[8,1,32,256,32]{3,2,4,1,0:T(8,128)(2,1)}), bf16[8,1,32,256,32]{3,2,4,1,0:T(8,128)(2,1)}, u32[]{:S(2)}, u32[]{:S(2)}) %all-to-all-start) | async-done | bytes 4194336 | tf_op jit(solution)/shard_map/all_to_all | solution.py:14
  151.3 5.1 all-to-all-start.1
  156.5 1.0 fusion.67
  157.6 1.0 fusion.68
  158.8 2.6 copy.53
  161.4 4.8 fusion.58
  166.2 4.8 fusion.50
  171.0 12.1 %fusion.55 = f32[32,256,256]{2,1,0:T(8,128)} fusion(f32[256,32,256]{2,0,1:T(8,128)S(1)} %fusion.58, f32[256,32,256]{2,0,1:T(8,128)S(1)} %fusion.50, f32[256,256]{1,0:T(8,128)S(1)} %copy.55, f32[256,256]{1,0:T(8,128)S(1)} %copy.54, pred[32]{0:T(512)(128)(4,1)S(1)} %dynamic-slice_compare_fusion), kind=kOutput, calls=%fused_computation.84 | convolution fusion | flops 6458048512 | bytes 25690144 | tf_op jit(solution)/shard_map/xmdb,bc->xmdc/dot_general | solution.py:22
  183.1 11.6 %fusion.46 = f32[32,256,256]{2,1,0:T(8,128)} fusion(f32[256,32,256]{2,0,1:T(8,128)S(1)} %fusion.58, f32[256,32,256]{2,0,1:T(8,128)S(1)} %fusion.50, f32[256,256]{1,0:T(8,128)S(1)} %copy.55, f32[256,256]{1,0:T(8,128)S(1)} %copy.54, pred[32]{0:T(512)(128)(4,1)S(1)} %dynamic-slice_compare_fusion), kind=kOutput, calls=%fused_computation.75 | convolution fusion | flops 6458048512 | bytes 25690144 | tf_op jit(solution)/shard_map/xmdb,bc->xmdc/dot_general | solution.py:22
  194.7 14.4 %multiply_subtract_fusion = f32[32,256,256]{2,1,0:T(8,128)} fusion(f32[32,256,256]{2,1,0:T(8,128)} %fusion.55, f32[256,32,256]{2,0,1:T(8,128)S(1)} %fusion.58, f32[256,32,256]{2,0,1:T(8,128)S(1)} %fusion.50, f32[256,256]{1,0:T(8,128)S(1)} %copy.55, f32[256,256]{1,0:T(8,128)S(1)} %copy.54, pred[32]{0:T(512)(128)(4,1)S(1)} %dynamic-slice_compare_fusion), kind=kOutput, calls=%fused_computation.38 | convolution fusion | flops 6462242816 | bytes 34078752 | tf_op jit(solution)/shard_map/xmdb,bc->xmdc/dot_general | solution.py:22
  209.1 129.6 %all-to-all-done.1 = bf16[2,32,256,256]{2,1,0,3:T(8,128)(2,1)} async-done(((bf16[2,32,256,256]{2,1,0,3:T(8,128)(2,1)}), bf16[2,32,256,256]{2,1,0,3:T(8,128)(2,1)}, u32[]{:S(2)}, u32[]{:S(2)}) %all-to-all-start.1) | async-done | bytes 8388640 | tf_op jit(solution)/shard_map/all_to_all | solution.py:84
  338.7 11.4 %copy.59 = bf16[2,32,256,256]{2,3,1,0:T(8,128)(2,1)} copy(bf16[2,32,256,256]{2,1,0,3:T(8,128)(2,1)} %all-to-all-done.1) | data formatting | bytes 16777216 | tf_op jit(solution)/shard_map/all_to_all | solution.py:84
  350.1 11.4 %convert_bitcast_fusion = f32[2,8,32,256,32]{3,4,1,2,0:T(8,128)} fusion(bf16[2,32,256,8,32]{2,4,3,1,0:T(8,128)(2,1)} %bitcast.152), kind=kLoop, calls=%fused_computation | loop fusion | flops 4194304 | bytes 25165824 | tf_op jit(solution)/shard_map/transpose | solution.py:91
  361.5 17.8 %copy.60 = f32[2,8,32,256,32]{3,2,1,4,0:T(8,128)} copy(f32[2,8,32,256,32]{3,4,1,2,0:T(8,128)} %convert_bitcast_fusion) | data formatting | bytes 33554432 | tf_op jit(solution)/shard_map/transpose | solution.py:91
  379.2 27.1 %fusion.19 = (f32[1,32,256,256]{3,2,1,0:T(8,128)}, f32[1,32,256,256]{3,2,1,0:T(8,128)}) fusion(f32[32,256,256]{2,1,0:T(8,128)} %multiply_subtract_fusion, f32[2,32,256,256]{3,2,1,0:T(8,128)} %bitcast.151, f32[256,32,256]{2,0,1:T(8,128)} %copy-done.1, f32[256,32,256]{2,0,1:T(8,128)} %copy-done.2, f32[256,256]{1,0:T(8,128)S(1)} %copy.55, ...), kind=kOutput, calls=%fused_computation.29 | convolution fusion | flops 6474825728 | bytes 67633184 | tf_op jit(solution)/shard_map/xmdb,bc->xmdc/dot_general | solution.py:22
  406.4 13.2 %fusion.14 = f32[32,256,256]{2,1,0:T(8,128)} fusion(f32[1,32,256,256]{3,2,1,0:T(8,128)} %get-tuple-element.6), kind=kOutput, calls=%fused_computation.22 | convolution fusion | flops 6443368448 | bytes 16777216 | tf_op jit(solution)/shard_map/xmdc,cb->xmdb/dot_general | solution.py:22
  419.6 11.2 %fusion.16 = f32[32,256,256]{2,1,0:T(8,128)} fusion(f32[1,32,256,256]{3,2,1,0:T(8,128)S(1)} %copy-done.3), kind=kOutput, calls=%fused_computation.24 | convolution fusion | flops 6443368448 | bytes 16777216 | tf_op jit(solution)/shard_map/xmdc,cb->xmdb/dot_general | solution.py:22
  430.8 10.8 %fusion.10 = f32[32,256,256]{2,1,0:T(8,128)} fusion(f32[1,32,256,256]{3,2,1,0:T(8,128)S(1)} %bitcast.148), kind=kOutput, calls=%fused_computation.18 | convolution fusion | flops 6443368448 | bytes 16777216 | tf_op jit(solution)/shard_map/xmdc,cb->xmdb/dot_general | solution.py:22
  441.7 11.0 %fusion.12 = f32[32,256,256]{2,1,0:T(8,128)} fusion(f32[1,32,256,256]{3,2,1,0:T(8,128)S(1)} %bitcast.148), kind=kOutput, calls=%fused_computation.20 | convolution fusion | flops 6443368448 | bytes 16777216 | tf_op jit(solution)/shard_map/xmdc,cb->xmdb/dot_general | solution.py:22
  452.7 19.1 %fusion.5 = f32[256,32,256]{2,0,1:T(8,128)} fusion(f32[256,256]{1,0:T(8,128)S(1)} %copy.55, f32[256,256]{1,0:T(8,128)S(1)} %copy.54, pred[32]{0:T(512)(128)(4,1)S(1)} %dynamic-slice_compare_fusion, f32[32,256,256]{2,1,0:T(8,128)} %fusion.14, f32[32,256,256]{2,1,0:T(8,128)} %fusion.10, f32[32,256,256]{2,1,0:T(8,128)} %fusion.16, f32[32,256,256]{2,1,0:T(8,128)} %fusion.12), kind=kOutput, calls=%fused_computation.15 | convolution fusion | flops 6458048512 | bytes 42467360 | tf_op jit(solution)/shard_map/xmdb,da->xmab/dot_general | solution.py:22
  471.8 20.9 %fusion.20 = bf16[1,256,256,32]{2,1,3,0:T(8,128)(2,1)} fusion(f32[256,32,256]{2,0,1:T(8,128)} %fusion.5, f32[256,256]{1,0:T(8,128)S(1)} %copy.55, f32[256,256]{1,0:T(8,128)S(1)} %copy.54, pred[32]{0:T(512)(128)(4,1)S(1)} %dynamic-slice_compare_fusion, f32[32,256,256]{2,1,0:T(8,128)} %fusion.14, f32[32,256,256]{2,1,0:T(8,128)} %fusion.10, ...), kind=kOutput, calls=%fused_computation.39 | convolution fusion | flops 6464339968 | bytes 46661664 | tf_op jit(solution)/shard_map/xmdb,da->xmab/dot_general | solution.py:22
  492.7 6.6 copy.69
  499.3 4.6 all-to-all-start.2
  503.9 9.2 %copy.71 = f32[1,8192,256]{1,2,0:T(8,128)} copy(f32[1,8192,256]{2,1,0:T(8,128)} %param.5) | data formatting | bytes 16777216 | tf_op args[0]
  513.1 83.2 %all-to-all-done.2 = bf16[1,256,256,32]{2,3,0,1:T(8,128)(2,1)} async-done(((bf16[1,256,256,32]{2,3,0,1:T(8,128)(2,1)}), bf16[1,256,256,32]{2,3,0,1:T(8,128)(2,1)}, u32[]{:S(2)}, u32[]{:S(2)}) %all-to-all-start.2) | async-done | bytes 4194336 | tf_op jit(solution)/shard_map/all_to_all | solution.py:113
  596.3 8.0 %copy.98 = f32[1,8,32,256,32]{3,2,4,1,0:T(8,128)} copy(bf16[1,8,32,256,32]{3,4,2,1,0:T(8,128)(2,1)} %bitcast.49) | data formatting | bytes 12582912 | tf_op jit(solution)/shard_map/convert_element_type | solution.py:115
  604.4 9.4 %reshape.158 = f32[1,8192,256]{1,2,0:T(8,128)} reshape(f32[1,32,256,8,32]{2,1,4,3,0:T(8,128)} %bitcast.153) | data formatting | bytes 16777216 | tf_op jit(solution)/shard_map/convert_element_type | solution.py:115
  613.8 16.1 %convert_bitcast_fusion.1 = bf16[1,8192,1024]{2,1,0:T(8,128)(2,1)} fusion(bf16[256,1024]{1,0:T(8,128)(2,1)S(1)} %copy-done, f32[1,8192,256]{1,2,0:T(8,128)} %reshape.158, f32[1,8192,256]{1,2,0:T(8,128)} %copy.71, f32[256]{0:T(256)S(1)} %copy-done.4), kind=kOutput, calls=%fused_computation.1 | convolution fusion | flops 4309647360 | bytes 34079744 | tf_op jit(solution)/shard_map/xtc,cj->xtj/dot_general | solution.py:122
  629.9 124.0 %reduce-scatter.2.cloned.1.call-done = bf16[1,8192,256]{2,1,0:T(8,128)(2,1)} async-done(((bf16[1,8192,1024]{2,1,0:T(8,128)(2,1)}), bf16[1,8192,256]{2,1,0:T(8,128)(2,1)}) %reduce-scatter.2.cloned.1.call-update) | async-done | bytes 4194320 | tf_op jit(solution)/shard_map/reduce_scatter | solution.py:123
  754.0 6.2 convert_element_type.130
  (24 shorter events, 2.1 us)
Async XLA Ops:
  6.5 607.2 %copy-start = (bf16[256,1024]{1,0:T(8,128)(2,1)S(1)}, bf16[256,1024]{1,0:T(8,128)(2,1)}, u32[]{:S(2)}) copy-start(bf16[256,1024]{1,0:T(8,128)(2,1)} %param.9) | copy-start | bytes 1572868
  50.7 100.6 %all-to-all-start = ((bf16[8,1,32,256,32]{3,2,4,1,0:T(8,128)(2,1)}), bf16[8,1,32,256,32]{3,2,4,1,0:T(8,128)(2,1)}, u32[]{:S(2)}, u32[]{:S(2)}) async-start(bf16[8,1,32,256,32]{3,2,4,1,0:T(8,128)(2,1)} %bitcast_dynamic-update-slice_fusion), calls=%async_computation | async-start | bytes 8388608 | tf_op jit(solution)/shard_map/all_to_all | solution.py:14
  74.9 83.8 %copy-start.5 = (s32[256]{0:T(256)S(1)}, s32[256]{0:T(256)}, u32[]{:S(2)}) copy-start(s32[256]{0:T(256)} %param.7) | copy-start | bytes 3076
  151.3 187.4 %all-to-all-start.1 = ((bf16[2,32,256,256]{2,1,0,3:T(8,128)(2,1)}), bf16[2,32,256,256]{2,1,0,3:T(8,128)(2,1)}, u32[]{:S(2)}, u32[]{:S(2)}) async-start(bf16[2,32,256,256]{2,1,0,3:T(8,128)(2,1)} %copy.58), calls=%async_computation.1 | async-start | bytes 16777216 | tf_op jit(solution)/shard_map/all_to_all | solution.py:84
  166.2 28.5 %copy-start.1 = (f32[256,32,256]{2,0,1:T(8,128)}, f32[256,32,256]{2,0,1:T(8,128)S(1)}, u32[]{:S(2)}) copy-start(f32[256,32,256]{2,0,1:T(8,128)S(1)} %fusion.58) | copy-start | bytes 25165828
  171.0 23.7 %copy-start.2 = (f32[256,32,256]{2,0,1:T(8,128)}, f32[256,32,256]{2,0,1:T(8,128)S(1)}, u32[]{:S(2)}) copy-start(f32[256,32,256]{2,0,1:T(8,128)S(1)} %fusion.50) | copy-start | bytes 25165828
  406.4 13.2 %copy-start.3 = (f32[1,32,256,256]{3,2,1,0:T(8,128)S(1)}, f32[1,32,256,256]{3,2,1,0:T(8,128)}, u32[]{:S(2)}) copy-start(f32[1,32,256,256]{3,2,1,0:T(8,128)} %get-tuple-element.6) | copy-start | bytes 25165828
  406.4 24.5 %slice-start = ((s8[8388608]{0:T(1024)(128)(4,1)}), s8[4194304]{0:T(1024)(128)(4,1)S(1)}, s32[]{:S(2)}) async-start(s8[8388608]{0:T(1024)(128)(4,1)} %bitcast.147), calls=%async_computation.5 | async-start | bytes 8388608
  419.6 11.2 %slice-start.1 = ((s8[8388608]{0:T(1024)(128)(4,1)}), s8[4194304]{0:T(1024)(128)(4,1)S(1)}, s32[]{:S(2)}) async-start(s8[8388608]{0:T(1024)(128)(4,1)} %bitcast.147), calls=%async_computation.6 | async-start | bytes 8388608
  499.3 97.0 %all-to-all-start.2 = ((bf16[1,256,256,32]{2,3,0,1:T(8,128)(2,1)}), bf16[1,256,256,32]{2,3,0,1:T(8,128)(2,1)}, u32[]{:S(2)}, u32[]{:S(2)}) async-start(bf16[1,256,256,32]{2,3,0,1:T(8,128)(2,1)} %copy.69), calls=%async_computation.2 | async-start | bytes 8388608 | tf_op jit(solution)/shard_map/all_to_all | solution.py:113
  503.9 250.1 %reduce-scatter.2.cloned.1.call-start = ((), (), s32[]{:S(2)}) async-start(), calls=%async_computation.4 | async-start | bytes 20971520 | tf_op jit(solution)/shard_map/reduce_scatter | solution.py:123
  604.4 9.4 %copy-start.4 = (f32[256]{0:T(256)S(1)}, f32[256]{0:T(256)}, u32[]{:S(2)}) copy-start(f32[256]{0:T(256)} %param.8) | copy-start | bytes 3076
Sparse Core Ops, SparseCore 0:
  630.0 123.8 reduce-scatter.1
